TPU v7x, 32 devices: a whole 2x2x4 slice. The times are simulated.
32 devices in a mesh: fsdp: 2 (over y), ctx: 4 (over x, core), tp: 4 (over z).
Axes of the slice: x: 2, y: 2, z: 4, core: 2. Of those that a mesh axis runs over, the one named last changes fastest.
Arguments:
- block_input: bfloat16 [4, 2048, 1024], P('fsdp', 'ctx'), may hold values from -6 to 6
- positions: int32 [3, 4, 2048], P(None, 'fsdp', 'ctx'), may hold values from 0 to 15
- w_qkv: bfloat16 [3, 1024, 1024], P(None, 'fsdp', 'tp'), may hold values from -0.1875 to 0.1875
- b_qkv: float32 [3, 1024], P(None, 'tp'), may hold values from -3 to 3
- w_proj: bfloat16 [1024, 1024], P('tp', 'fsdp'), may hold values from -1 to 1
- w_up: bfloat16 [1024, 4096], P('fsdp', 'tp'), may hold values from -0.1875 to 0.1875
- b_up: float32 [4096], P('tp'), may hold values from -3 to 3
- w_down: bfloat16 [4096, 1024], P('tp', 'fsdp'), may hold values from -0.09375 to 0.09375
- norm_gains: float32 [2, 1024], replicated, may hold values from 0.5 to 1.5
- norm_shifts: float32 [2, 1024], replicated, may hold values from -2 to 2
- out_shifts: float32 [2, 1024], replicated, may hold values from -2 to 2
- grad_out: bfloat16 [4, 2048, 1024], P('fsdp', 'ctx'), may hold values from -6 to 6
Outputs:
- block_output: bfloat16 [4, 2048, 1024], P('fsdp', 'ctx')
- grad_input: float32 [4, 2048, 1024], P('fsdp', 'ctx')
- grad_w_qkv: float32 [3, 1024, 1024], P(None, 'fsdp', 'tp')
- grad_b_qkv: float32 [3, 1024], P(None, 'tp')
- grad_w_proj: float32 [1024, 1024], P('tp', 'fsdp')
- grad_w_up: float32 [1024, 4096], P('fsdp', 'tp')
- grad_b_up: float32 [4096], P('tp')
- grad_w_down: float32 [4096, 1024], P('tp', 'fsdp')
- grad_gains: float32 [2, 1024], replicated
- grad_shifts: float32 [2, 1024], replicated
- grad_out_shifts: float32 [2, 1024], replicated
Inputs may be any that keep to these rules, and one draw needn't show every extreme that they name: `positions`: each token's time, height and width index in its clip.
All inputs are finite; a program needn't handle non-finite values.
Results may differ from a plain program's by a relative error of at most 0.02.
Values may be sent and summed in bfloat16 or wider, within the bound.
A program may use at most 128 MiB of HBM per device.

v0:
```python
from functools import partial
import jax
import jax.numpy as jnp
from jax import lax
from jax.sharding import PartitionSpec as P

HD = 64
LEN = 2048
ROT = 20
QBLK = 512
EPSILON = 1e-06


def layer_norm(values, gain_vec, shift_vec):
    center = values - jnp.mean(values, axis=-1, keepdims=True)
    spread = jnp.mean(center * center, axis=-1, keepdims=True)
    return center * lax.rsqrt(spread + EPSILON) * gain_vec + shift_vec


def rotary_tables(position_rows):
    half_rot = ROT // 2
    freqs = 10000.0 ** (-2.0 * jnp.arange(half_rot, dtype=jnp.float32) / ROT)
    angles = position_rows.astype(jnp.float32)[:, :, None] * freqs[None, None, :]
    return (jnp.cos(angles), jnp.sin(angles))


def rotary(values, cos_table, sin_table):
    half_rot = ROT // 2
    pieces = []
    for dim_index in range(3):
        offset_at = dim_index * ROT
        first_half = values[..., offset_at : offset_at + half_rot]
        second_half = values[..., offset_at + half_rot : offset_at + ROT]
        cos_part = cos_table[dim_index][:, None, :]
        sin_part = sin_table[dim_index][:, None, :]
        pieces.append(first_half * cos_part - second_half * sin_part)
        pieces.append(second_half * cos_part + first_half * sin_part)
    pieces.append(values[..., 3 * ROT :])
    return jnp.concatenate(pieces, axis=-1)


def contract_rows(left_mat, right_mat):
    return lax.dot_general(
        left_mat, right_mat, (((0,), (0,)), ((), ())), preferred_element_type=jnp.float32
    )


def contract_cols(left_mat, right_mat):
    return lax.dot_general(
        left_mat, right_mat, (((1,), (1,)), ((), ())), preferred_element_type=jnp.float32
    )


def tp_whole(partial_sum):
    return lax.psum(partial_sum.astype(jnp.bfloat16), "tp").astype(jnp.float32)


def attend_group(operands):
    queries, keys_all, values_all = operands
    score_factor = HD ** (-0.5)

    def attend_block(query_block):
        scores = (
            jnp.einsum("qe,ke->qk", query_block, keys_all, preferred_element_type=jnp.float32)
            * score_factor
        )
        largest = jnp.max(scores, axis=-1, keepdims=True)
        expon = jnp.exp(scores - largest)
        totals = jnp.sum(expon, axis=-1, keepdims=True)
        probs = expon / totals
        block_out = jnp.dot(
            probs.astype(jnp.bfloat16), values_all, preferred_element_type=jnp.float32
        )
        return (block_out.astype(jnp.bfloat16), (largest + jnp.log(totals))[:, 0])

    return lax.map(attend_block, queries.reshape(LEN // QBLK, QBLK, HD))


def backward_group(operands):
    queries, keys_all, values_all, grad_attended, log_totals = operands
    score_factor = HD ** (-0.5)

    def back_block(carry, block_items):
        grad_keys, grad_values = carry
        query_block, grad_block, log_block = block_items
        scores = (
            jnp.einsum("qe,ke->qk", query_block, keys_all, preferred_element_type=jnp.float32)
            * score_factor
        )
        probs = jnp.exp(scores - log_block[:, None])
        probs_low = probs.astype(jnp.bfloat16)
        grad_probs = jnp.einsum(
            "qe,ke->qk", grad_block, values_all, preferred_element_type=jnp.float32
        )
        inner = jnp.sum(probs * grad_probs, axis=-1, keepdims=True)
        grad_scores = (probs * (grad_probs - inner)).astype(jnp.bfloat16)
        grad_query = (
            jnp.dot(grad_scores, keys_all, preferred_element_type=jnp.float32) * score_factor
        )
        grad_keys = grad_keys + contract_rows(grad_scores, query_block) * score_factor
        grad_values = grad_values + contract_rows(probs_low, grad_block)
        return ((grad_keys, grad_values), grad_query)

    zeros_kv = jnp.zeros((LEN, HD), jnp.float32)
    block_count = LEN // QBLK
    items = (
        queries.reshape(block_count, QBLK, HD),
        grad_attended.reshape(block_count, QBLK, HD),
        log_totals,
    )
    (grad_keys, grad_values), grad_queries = lax.scan(back_block, (zeros_kv, zeros_kv), items)
    return (grad_queries.reshape(LEN, HD), grad_keys, grad_values)


def shards(
    block_input,
    positions,
    w_qkv,
    b_qkv,
    w_proj,
    w_up,
    b_up,
    w_down,
    norm_gains,
    norm_shifts,
    out_shifts,
    grad_out,
):
    clip_count, local_len, width = block_input.shape
    row_count = clip_count * local_len
    ctx_count = lax.axis_size("ctx")
    local_width = w_qkv.shape[2]
    group_heads = local_width // ctx_count // HD
    group_count = clip_count * group_heads
    inputs = block_input.reshape(row_count, width).astype(jnp.float32)
    full_qkv, full_proj, full_up, full_down = (
        lax.all_gather(w_qkv, "fsdp", axis=1, tiled=True),
        lax.all_gather(w_proj, "fsdp", axis=1, tiled=True),
        lax.all_gather(w_up, "fsdp", axis=0, tiled=True),
        lax.all_gather(w_down, "fsdp", axis=1, tiled=True),
    )
    cos_table, sin_table = rotary_tables(positions.reshape(3, row_count))
    normed_one = layer_norm(inputs, norm_gains[0], norm_shifts[0])
    normed_one_low = normed_one.astype(jnp.bfloat16)
    projected = (
        jnp.einsum("rd,cde->cre", normed_one_low, full_qkv, preferred_element_type=jnp.float32)
        + b_qkv[:, None, :]
    )
    head_shape = (row_count, local_width // HD, HD)
    queries_rot = rotary(projected[0].reshape(head_shape), cos_table, sin_table).reshape(
        row_count, local_width
    )
    keys_rot = rotary(projected[1].reshape(head_shape), cos_table, sin_table).reshape(
        row_count, local_width
    )
    token_qkv = (
        jnp.stack([queries_rot, keys_rot, projected[2]])
        .astype(jnp.bfloat16)
        .reshape(3, clip_count, local_len, local_width)
    )
    head_qkv = lax.all_to_all(token_qkv, "ctx", split_axis=3, concat_axis=2, tiled=True)
    full_len = head_qkv.shape[2]
    grouped = (
        head_qkv.reshape(3, clip_count, full_len, group_heads, HD)
        .transpose(0, 1, 3, 2, 4)
        .reshape(3, group_count, full_len, HD)
    )
    attended, log_totals = lax.map(attend_group, (grouped[0], grouped[1], grouped[2]))
    attended = (
        attended.reshape(clip_count, group_heads, full_len, HD)
        .transpose(0, 2, 1, 3)
        .reshape(clip_count, full_len, group_heads * HD)
    )
    token_attended = lax.all_to_all(
        attended, "ctx", split_axis=1, concat_axis=2, tiled=True
    ).reshape(row_count, local_width)
    attn_part = jnp.dot(token_attended, full_proj, preferred_element_type=jnp.float32)
    residual = inputs + tp_whole(attn_part) + out_shifts[0]
    normed_two_low = layer_norm(residual, norm_gains[1], norm_shifts[1]).astype(jnp.bfloat16)
    pre_act = jnp.dot(normed_two_low, full_up, preferred_element_type=jnp.float32) + b_up
    act_low = jax.nn.gelu(pre_act, approximate=False).astype(jnp.bfloat16)
    mlp_part = jnp.dot(act_low, full_down, preferred_element_type=jnp.float32)
    result = residual + tp_whole(mlp_part) + out_shifts[1]
    block_rows = result.astype(jnp.bfloat16)
    full_qkv, full_proj, full_up, full_down = (
        lax.all_gather(w_qkv, "fsdp", axis=1, tiled=True),
        lax.all_gather(w_proj, "fsdp", axis=1, tiled=True),
        lax.all_gather(w_up, "fsdp", axis=0, tiled=True),
        lax.all_gather(w_down, "fsdp", axis=1, tiled=True),
    )
    upstream = grad_out.reshape(row_count, width).astype(jnp.float32)
    upstream_low = upstream.astype(jnp.bfloat16)
    grad_down = contract_rows(act_low, upstream_low)
    grad_act = contract_cols(upstream_low, full_down)
    _, gelu_pull = jax.vjp(partial(jax.nn.gelu, approximate=False), pre_act)
    grad_pre = gelu_pull(grad_act)[0].astype(jnp.bfloat16)
    grad_b_up = jnp.sum(grad_pre.astype(jnp.float32), axis=0)
    grad_up = contract_rows(normed_two_low, grad_pre)
    back_part_two = contract_cols(grad_pre, full_up)
    grad_normed_two = tp_whole(back_part_two)
    _, norm_pull_two = jax.vjp(layer_norm, residual, norm_gains[1], norm_shifts[1])
    grad_res_norm, grad_gain_two, grad_shift_two = norm_pull_two(grad_normed_two)
    grad_residual = upstream + grad_res_norm
    grad_residual_low = grad_residual.astype(jnp.bfloat16)
    grad_proj = contract_rows(token_attended, grad_residual_low)
    grad_token_att = (
        contract_cols(grad_residual_low, full_proj)
        .astype(jnp.bfloat16)
        .reshape(clip_count, local_len, local_width)
    )
    grad_head_att = lax.all_to_all(grad_token_att, "ctx", split_axis=2, concat_axis=1, tiled=True)
    grad_grouped = (
        grad_head_att.reshape(clip_count, full_len, group_heads, HD)
        .transpose(0, 2, 1, 3)
        .reshape(group_count, full_len, HD)
    )
    grad_q, grad_k, grad_v = lax.map(
        backward_group, (grouped[0], grouped[1], grouped[2], grad_grouped, log_totals)
    )
    grad_heads = jnp.stack([grad_q, grad_k, grad_v]).astype(jnp.bfloat16)
    grad_heads = (
        grad_heads.reshape(3, clip_count, group_heads, full_len, HD)
        .transpose(0, 1, 3, 2, 4)
        .reshape(3, clip_count, full_len, group_heads * HD)
    )
    grad_tokens = (
        lax.all_to_all(grad_heads, "ctx", split_axis=2, concat_axis=3, tiled=True)
        .reshape(3, row_count, local_width)
        .astype(jnp.float32)
    )

    def rotate_rows(moved):
        return rotary(moved, cos_table, sin_table)

    _, rotary_pull = jax.vjp(rotate_rows, jnp.zeros(head_shape, jnp.float32))
    grad_q_pre = rotary_pull(grad_tokens[0].reshape(head_shape))[0].reshape(row_count, local_width)
    grad_k_pre = rotary_pull(grad_tokens[1].reshape(head_shape))[0].reshape(row_count, local_width)
    grad_qkv_low = jnp.stack([grad_q_pre, grad_k_pre, grad_tokens[2]]).astype(jnp.bfloat16)
    grad_b_qkv = jnp.sum(grad_qkv_low.astype(jnp.float32), axis=1)
    grad_qkv = jnp.einsum(
        "rd,cre->cde", normed_one_low, grad_qkv_low, preferred_element_type=jnp.float32
    )
    back_part_one = jnp.einsum(
        "cre,cde->rd", grad_qkv_low, full_qkv, preferred_element_type=jnp.float32
    )
    grad_normed_one = tp_whole(back_part_one)
    _, norm_pull_one = jax.vjp(layer_norm, inputs, norm_gains[0], norm_shifts[0])
    grad_in_norm, grad_gain_one, grad_shift_one = norm_pull_one(grad_normed_one)
    grad_input_rows = grad_residual + grad_in_norm
    norm_vectors = jnp.stack(
        [
            grad_gain_one,
            grad_gain_two,
            grad_shift_one,
            grad_shift_two,
            jnp.sum(grad_residual, axis=0),
            jnp.sum(upstream, axis=0),
        ]
    )
    block_output = block_rows.reshape(clip_count, local_len, width)
    grad_input = grad_input_rows.reshape(clip_count, local_len, width)
    shard_qkv, shard_proj, shard_up, shard_down = (
        lax.psum_scatter(
            grad_qkv.astype(jnp.bfloat16), "fsdp", scatter_dimension=1, tiled=True
        ).astype(jnp.float32),
        lax.psum_scatter(
            grad_proj.astype(jnp.bfloat16), "fsdp", scatter_dimension=1, tiled=True
        ).astype(jnp.float32),
        lax.psum_scatter(
            grad_up.astype(jnp.bfloat16), "fsdp", scatter_dimension=0, tiled=True
        ).astype(jnp.float32),
        lax.psum_scatter(
            grad_down.astype(jnp.bfloat16), "fsdp", scatter_dimension=1, tiled=True
        ).astype(jnp.float32),
    )
    shard_qkv, shard_proj, shard_up, shard_down = (
        lax.psum(shard_qkv.astype(jnp.bfloat16), "ctx").astype(jnp.float32),
        lax.psum(shard_proj.astype(jnp.bfloat16), "ctx").astype(jnp.float32),
        lax.psum(shard_up.astype(jnp.bfloat16), "ctx").astype(jnp.float32),
        lax.psum(shard_down.astype(jnp.bfloat16), "ctx").astype(jnp.float32),
    )
    gains_sum, shifts_sum, outs_sum, bqkv_sum, bup_sum = lax.psum(
        (norm_vectors[0:2], norm_vectors[2:4], norm_vectors[4:6], grad_b_qkv, grad_b_up),
        ("fsdp", "ctx"),
    )
    return (
        block_output,
        grad_input,
        shard_qkv,
        bqkv_sum,
        shard_proj,
        shard_up,
        bup_sum,
        shard_down,
        gains_sum,
        shifts_sum,
        outs_sum,
    )


def solution(mesh):
    in_specs = (
        P("fsdp", "ctx", None),
        P(None, "fsdp", "ctx"),
        P(None, "fsdp", "tp"),
        P(None, "tp"),
        P("tp", "fsdp"),
        P("fsdp", "tp"),
        P("tp"),
        P("tp", "fsdp"),
        P(),
        P(),
        P(),
        P("fsdp", "ctx", None),
    )
    out_specs = (
        P("fsdp", "ctx", None),
        P("fsdp", "ctx", None),
        P(None, "fsdp", "tp"),
        P(None, "tp"),
        P("tp", "fsdp"),
        P("fsdp", "tp"),
        P("tp"),
        P("tp", "fsdp"),
        P(),
        P(),
        P(),
    )
    return jax.shard_map(shards, mesh=mesh, in_specs=in_specs, out_specs=out_specs, check_vma=False)
```

profile of v0, /device:TPU:0, one launch (start us, length us, event | category | flops | bytes accessed | tf_op | source)
XLA Modules:
  0.0 875.1 jit_solution(13437522062420596701)
XLA Ops:
  17.3 22.8 %all-gather.4.cloned.1.call-done = bf16[3,1024,256]{1,2,0:T(8,128)(2,1)} async-done(((bf16[3,512,256]{1,2,0:T(8,128)(2,1)}), bf16[3,1024,256]{1,2,0:T(8,128)(2,1)}) %all-gather.4.cloned.1.call-update) | async-done | bytes 1572880 | tf_op jit(solution)/shard_map/all_gather | solution.py:137
  40.1 3.9 add_bitcast_fusion
  51.5 3.1 pad_maximum_fusion.1
  54.5 3.8 all-to-all-start
  58.3 20.0 %all-to-all-done = bf16[3,2,512,256]{2,1,0,3:T(2,128)(2,1)S(1)} async-done(((bf16[3,2,512,256]{2,1,0,3:T(2,128)(2,1)}), bf16[3,2,512,256]{2,1,0,3:T(2,128)(2,1)S(1)}, u32[]{:S(2)}, u32[]{:S(2)}) %all-to-all-start) | async-done | bytes 1572896 | tf_op jit(solution)/shard_map/all_to_all | solution.py:161
  83.0 27.2 %while.54 = (s32[]{:T(128)}, bf16[2,4,512,64]{2,3,1,0:T(8,128)(2,1)}, f32[2,4,512]{2,1,0:T(4,128)S(1)}, bf16[2,2048,64]{2,1,0:T(8,128)(2,1)S(1)}, bf16[2,2048,64...) while((s32[]{:T(128)}, ...), condition=%wide.region_7.8_spmd, body=%wide.region_2.7_spmd.sunk | while | flops 277904896 | bytes 20156772 | solution.py:168
  84.4 11.4 %while.57 = (s32[]{:T(128)}, bf16[4,512,64]{1,2,0:T(8,128)(2,1)S(1)}, f32[4,512]{1,0:T(4,128)S(1)}, bf16[4,512,64]{2,1,0:T(8,128)(2,1)S(1)}, bf16[2048,64]{1,0:T...) while((s32[]{:T(128)}, bf16[4,512,64]{1,2,0:T(8,128)(2,1)S(1)}, ...), condition=%wide.region_6.6_spmd, body=%wide.region_3.5_spmd.sunk | while | flops 277904896 | bytes 13848681 | solution.py:76
  98.0 11.4 %while.57 = (s32[]{:T(128)}, bf16[4,512,64]{1,2,0:T(8,128)(2,1)S(1)}, f32[4,512]{1,0:T(4,128)S(1)}, bf16[4,512,64]{2,1,0:T(8,128)(2,1)S(1)}, bf16[2048,64]{1,0:T...) while((s32[]{:T(128)}, bf16[4,512,64]{1,2,0:T(8,128)(2,1)S(1)}, ...), condition=%wide.region_6.6_spmd, body=%wide.region_3.5_spmd.sunk | while | flops 277904896 | bytes 13848681 | solution.py:76
  114.4 3.5 all-to-all-start.1
  117.9 9.3 %all_gather.17 = bf16[256,1024]{1,0:T(8,128)(2,1)S(1)} all-gather(bf16[256,512]{1,0:T(8,128)(2,1)S(1)} %copy-done.30), channel_id=1, replica_groups=mesh['fsdp'=2,'ctx'=4,'tp'=4] {'fsdp'}, dimensions={1}, use_global_device_ids=true | all-gather | bytes 786432 | tf_op jit(solution)/shard_map/all_gather | solution.py:138
  135.5 84.2 %all-reduce.22.cloned.1.call-done = bf16[1024,1024]{1,0:T(8,128)(2,1)} async-done(((bf16[1024,1024]{1,0:T(8,128)(2,1)}), bf16[1024,1024]{1,0:T(8,128)(2,1)}) %all-reduce.22.cloned.1.call-update) | async-done | bytes 2097168 | tf_op jit(solution)/shard_map/psum | solution.py:55
  222.2 3.0 multiply_reduce_fusion.2
  225.3 28.2 %all-gather.6.cloned.1.call-done = bf16[1024,1024]{1,0:T(8,128)(2,1)} async-done(((bf16[512,1024]{1,0:T(8,128)(2,1)}), bf16[1024,1024]{1,0:T(8,128)(2,1)}) %all-gather.6.cloned.1.call-update) | async-done | bytes 2097168 | tf_op jit(solution)/shard_map/all_gather | solution.py:139
  253.4 7.4 fusion.69
  260.8 27.1 %all-gather.8.cloned.1.call-done = bf16[1024,1024]{1,0:T(8,128)(2,1)} async-done(((bf16[1024,512]{1,0:T(8,128)(2,1)}), bf16[1024,1024]{1,0:T(8,128)(2,1)}) %all-gather.8.cloned.1.call-update) | async-done | bytes 2097168 | tf_op jit(solution)/shard_map/all_gather | solution.py:140
  287.9 16.0 %convert_reduce_fusion.4 = (f32[1024]{0:T(1024)}, bf16[1024,1024]{1,0:T(8,128)(2,1)S(1)}, f32[1024,1024]{1,0:T(8,128)}) fusion(f32[1024,1024]{1,0:T(8,128)} %fusion.69, f32[1024]{0:T(1024)S(1)} %copy-done.50, bf16[1024,1024]{1,0:T(8,128)(2,1)S(1)} %bitcast.274, bf16[1024,1024]{1,0:T(8,128)(2,1)} %all-gather.8.cloned.1.call-done), kind=kOutput, calls=%fused_computation.82 | convolution fusion | flops 2226125824 | bytes 14688256 | tf_op jit(solution)/shard_map/dot_general | solution.py:49
  305.2 3.7 convolution_convert_fusion.2
  308.9 12.1 %reduce-scatter.7.cloned.1.call-start = ((), (), s32[]{:S(2)}) async-start(), calls=%async_computation.14 | async-start | bytes 786432 | tf_op jit(solution)/shard_map/reduce_scatter | solution.py:266
  321.1 74.2 %all-reduce.24.cloned.1.call-done = bf16[1024,1024]{1,0:T(8,128)(2,1)} async-done(((bf16[1024,1024]{1,0:T(8,128)(2,1)}), bf16[1024,1024]{1,0:T(8,128)(2,1)}) %all-reduce.24.cloned.1.call-update) | async-done | bytes 2097168 | tf_op jit(solution)/shard_map/psum | solution.py:55
  395.3 4.5 convert_reduce_fusion.1
  408.6 4.6 multiply_convert_fusion.1
  414.5 3.8 convolution_convert_fusion
  418.3 3.0 convolution_convert_fusion.6
  422.5 3.5 all-to-all-start.2
  426.0 6.9 convolution_convert_fusion.1
  436.1 103.6 %while.56 = (s32[]{:T(128)}, bf16[2,2048,64]{2,0,1:T(2,128)(2,1)}, bf16[2,2048,64]{1,2,0:T(8,128)(2,1)}, bf16[2,2048,64]{1,2,0:T(8,128)(2,1)}, bf16[2,2048,64]{2...) while((s32[]{:T(128)}, bf16[2,2048,64]{2,0,1:T(2,128)(2,1)}, ...), condition=%wide.region_19.20_spmd, body=%wide.region_15.19_spmd.sunk | while | flops 680164864 | bytes 41838996 | solution.py:217
  440.5 20.1 %while.58 = (s32[]{:T(128)}, f32[2048,64]{0,1:T(8,128)S(1)}, f32[2048,64]{0,1:T(8,128)S(1)}, f32[4,512,64]{1,2,0:T(8,128)}, bf16[4,512,64]{2,1,0:T(8,128)(2,1)S(...) while((s32[]{:T(128)}, f32[2048,64]{0,1:T(8,128)S(1)}, ...), condition=%wide.region_18.18_spmd.clone, body=%wide.region_16.17_spmd.clone.sunk | while | flops 680164864 | bytes 35530900 | solution.py:111
  462.0 25.1 %dynamic_update_slice.47 = bf16[2,2048,64]{2,0,1:T(2,128)(2,1)} dynamic-update-slice(bf16[2,2048,64]{2,0,1:T(2,128)(2,1)} %get-tuple-element.795, f32[1,2048,64]{2,0,1:T(1,128)S(1)} %bitcast.268, s32[]{:T(128)S(6)} %copy.189, s32[]{:T(128)} %constant.78.clone.1..sunk.2, s32[]{:T(128)} %constant.78.clone.1..sunk.2) | dynamic-update-slice | bytes 1048580 | tf_op jit(solution)/shard_map/while/body/jit(dynamic_update_index_in_dim)/dynamic_update_slice | solution.py:217
  492.3 20.1 %while.58 = (s32[]{:T(128)}, f32[2048,64]{0,1:T(8,128)S(1)}, f32[2048,64]{0,1:T(8,128)S(1)}, f32[4,512,64]{1,2,0:T(8,128)}, bf16[4,512,64]{2,1,0:T(8,128)(2,1)S(...) while((s32[]{:T(128)}, f32[2048,64]{0,1:T(8,128)S(1)}, ...), condition=%wide.region_18.18_spmd.clone, body=%wide.region_16.17_spmd.clone.sunk | while | flops 680164864 | bytes 35530900 | solution.py:111
  513.8 25.1 %dynamic_update_slice.47 = bf16[2,2048,64]{2,0,1:T(2,128)(2,1)} dynamic-update-slice(bf16[2,2048,64]{2,0,1:T(2,128)(2,1)} %get-tuple-element.795, f32[1,2048,64]{2,0,1:T(1,128)S(1)} %bitcast.268, s32[]{:T(128)S(6)} %copy.189, s32[]{:T(128)} %constant.78.clone.1..sunk.2, s32[]{:T(128)} %constant.78.clone.1..sunk.2) | dynamic-update-slice | bytes 1048580 | tf_op jit(solution)/shard_map/while/body/jit(dynamic_update_index_in_dim)/dynamic_update_slice | solution.py:217
  539.7 3.6 copy.142
  543.3 3.6 copy.141
  546.8 7.2 fusion.79
  554.0 3.3 reshape.228
  557.3 24.7 %all_to_all.57 = bf16[4,2,98304]{2,1,0:T(2,128)(2,1)} all-to-all(bf16[4,2,98304]{2,1,0:T(2,128)(2,1)} %reshape.228), channel_id=1, replica_groups=mesh['fsdp'=2,'ctx'=4,'tp'=4] {'ctx'}, dimensions={0} | all-to-all | bytes 3145728 | tf_op jit(solution)/shard_map/all_to_all | solution.py:227
  582.0 3.8 reshape.229
  585.8 6.4 copy.92
  601.3 4.9 fusion.61
  606.3 5.4 convolution_convert_fusion.3
  611.7 3.1 bitcast_convert_fusion
  618.7 11.9 %reduce-scatter.5.cloned.1.call-done = bf16[3,512,256]{1,2,0:T(8,128)(2,1)} async-done(((bf16[3,1024,256]{1,2,0:T(8,128)(2,1)}), bf16[3,512,256]{1,2,0:T(8,128)(2,1)}) %reduce-scatter.5.cloned.1.call-update) | async-done | bytes 786448 | tf_op jit(solution)/shard_map/reduce_scatter | solution.py:263
  630.7 157.9 %all-reduce.26.cloned.1.call-done = (bf16[1024,1024]{1,0:T(8,128)(2,1)}, bf16[1024,1024]{1,0:T(8,128)(2,1)}) async-done(((bf16[1024,1024]{1,0:T(8,128)(2,1)}, bf16[1024,1024]{1,0:T(8,128)(2,1)}), (bf16[1024,1024]{1,0:T(8,128)(2,1)}, bf16[1024,1024]{1,0:T(8,128)(2,1)})) %all-reduce.26.cloned.1.call-update) | async-done | bytes 4194320 | tf_op jit(solution)/shard_map/psum | solution.py:55
  788.6 3.1 convert_reduce_fusion
  791.7 2.7 fusion.35
  794.5 26.2 %all-reduce.14 = (f32[3,256]{1,0:T(4,128)}, f32[1024]{0:T(1024)}, f32[2,1024]{1,0:T(2,128)}, f32[2,1024]{1,0:T(2,128)}, f32[2,1024]{1,0:T(2,128)}) all-reduce(f32[3,256]{1,0:T(4,128)S(1)} %convert_reduce_fusion.5, f32[1024]{0:T(1024)S(1)} %copy-done.52, ...), channel_id=1, replica_groups=mesh['fsdp'=2,'ctx'=4,'tp'=4] {'fsdp','ctx'}, use_global_device_ids=true, to_apply=%region_26.27 | all-reduce | flops 7936 | bytes 63488 | tf_op jit(solution)/shard_map/psum | solution.py:282
  820.7 7.1 add_add_fusion.2
  827.9 31.4 %all-reduce.28.cloned.1.call-done = (bf16[3,512,256]{1,2,0:T(8,128)(2,1)}, bf16[256,512]{1,0:T(8,128)(2,1)}, bf16[512,1024]{1,0:T(8,128)(2,1)}, bf16[1024,512]{1,0:T(8,128)(2,1)}) async-done(((bf16[3,512,256]{1,2,0:T(8,128)(2,1)}, bf16[256,512]{1,0:T(8,128)(2,1)}, bf16[512,1024]{1,0:T(8,128)(2,1)}, bf16[1024,512]{1,0:T(8,128)(2,1)}), (bf16[3,512,256]{1,2,0:T(8,128)(2,1)}, bf16[256,512]{1,0:T(8,128)(2,1)}, ...) | async-done | bytes 3145744 | tf_op jit(solution)/shard_map/psum | solution.py:277
  863.7 2.8 convert_element_type.170
  (351 shorter events, 151.5 us)
Async XLA Ops:
  7.2 5.3 copy-start.46
  7.2 5.8 copy-start.47
  7.2 6.4 copy-start.48
  7.2 32.9 %all-gather.4.cloned.1.call-start = ((), (), s32[]{:S(2)}) async-start(), calls=%async_computation.8 | async-start | bytes 2359296 | tf_op jit(solution)/shard_map/all_gather | solution.py:137
  11.7 28.4 %copy-start.55 = (f32[3,256]{1,0:T(4,128)S(1)}, f32[3,256]{1,0:T(4,128)}, u32[]{:S(2)}) copy-start(f32[3,256]{1,0:T(4,128)} %param.23) | copy-start | bytes 9220
  15.0 30.8 %copy-start.15 = (f32[1024,10]{0,1:T(8,128)}, f32[1024,10]{0,1:T(8,128)S(1)}, u32[]{:S(2)}) copy-start(f32[1024,10]{0,1:T(8,128)S(1)} %get-tuple-element.436) | copy-start | bytes 122884
  15.0 30.8 %copy-start.17 = (f32[1024,10]{0,1:T(8,128)}, f32[1024,10]{0,1:T(8,128)S(1)}, u32[]{:S(2)}) copy-start(f32[1024,10]{0,1:T(8,128)S(1)} %get-tuple-element.437) | copy-start | bytes 122884
  15.0 30.8 %copy-start.19 = (f32[1024,10]{0,1:T(8,128)}, f32[1024,10]{0,1:T(8,128)S(1)}, u32[]{:S(2)}) copy-start(f32[1024,10]{0,1:T(8,128)S(1)} %get-tuple-element.438) | copy-start | bytes 122884
  15.1 30.8 %copy-start.21 = (f32[1024,10]{0,1:T(8,128)}, f32[1024,10]{0,1:T(8,128)S(1)}, u32[]{:S(2)}) copy-start(f32[1024,10]{0,1:T(8,128)S(1)} %get-tuple-element.449) | copy-start | bytes 122884
  15.1 30.8 %copy-start.23 = (f32[1024,10]{0,1:T(8,128)}, f32[1024,10]{0,1:T(8,128)S(1)}, u32[]{:S(2)}) copy-start(f32[1024,10]{0,1:T(8,128)S(1)} %get-tuple-element.450) | copy-start | bytes 122884
  15.1 30.8 %copy-start.25 = (f32[1024,10]{0,1:T(8,128)}, f32[1024,10]{0,1:T(8,128)S(1)}, u32[]{:S(2)}) copy-start(f32[1024,10]{0,1:T(8,128)S(1)} %get-tuple-element.451) | copy-start | bytes 122884
  54.5 23.8 %all-to-all-start = ((bf16[3,2,512,256]{2,1,0,3:T(2,128)(2,1)}), bf16[3,2,512,256]{2,1,0,3:T(2,128)(2,1)S(1)}, u32[]{:S(2)}, u32[]{:S(2)}) async-start(bf16[3,2,512,256]{2,1,0,3:T(2,128)(2,1)} %pad_maximum_fusion.1), calls=%async_computation | async-start | bytes 3145728 | tf_op jit(solution)/shard_map/all_to_all | solution.py:161
  84.4 11.4 %copy-start.28 = (bf16[2,4,512,64]{2,3,1,0:T(8,128)(2,1)S(1)}, bf16[2,4,512,64]{2,3,1,0:T(8,128)(2,1)}, u32[]{:S(2)}) copy-start(bf16[2,4,512,64]{2,3,1,0:T(8,128)(2,1)} %get-tuple-element.762) | copy-start | bytes 1572868 | tf_op jit(solution)/shard_map/while
  98.0 11.4 %copy-start.28 = (bf16[2,4,512,64]{2,3,1,0:T(8,128)(2,1)S(1)}, bf16[2,4,512,64]{2,3,1,0:T(8,128)(2,1)}, u32[]{:S(2)}) copy-start(bf16[2,4,512,64]{2,3,1,0:T(8,128)(2,1)} %get-tuple-element.762) | copy-start | bytes 1572868 | tf_op jit(solution)/shard_map/while
  110.2 19.6 %copy-start.5 = (bf16[2,2048,64]{2,1,0:T(8,128)(2,1)}, bf16[2,2048,64]{2,1,0:T(8,128)(2,1)S(1)}, u32[]{:S(2)}) copy-start(bf16[2,2048,64]{2,1,0:T(8,128)(2,1)S(1)} %get-tuple-element.841) | copy-start | bytes 1572868
  110.3 7.7 copy-start.30
  114.4 12.8 %all-to-all-start.1 = ((bf16[4,2,32768]{2,1,0:T(2,128)(2,1)}), bf16[4,2,32768]{2,1,0:T(2,128)(2,1)S(1)}, u32[]{:S(2)}, u32[]{:S(2)}) async-start(bf16[4,2,32768]{2,1,0:T(2,128)(2,1)} %reshape.226), calls=%async_computation.1 | async-start | bytes 1048576 | tf_op jit(solution)/shard_map/all_to_all | solution.py:174
  117.9 101.8 %all-reduce.22.cloned.1.call-start = ((), (), s32[]{:S(2)}) async-start(), calls=%async_computation.9 | async-start | bytes 4194304 | tf_op jit(solution)/shard_map/psum | solution.py:55
  129.9 89.8 %copy-start.1 = (bf16[2,512,1024]{2,1,0:T(8,128)(2,1)S(1)}, bf16[2,512,1024]{2,1,0:T(8,128)(2,1)}, u32[]{:S(2)}) copy-start(bf16[2,512,1024]{2,1,0:T(8,128)(2,1)} %param.20) | copy-start | bytes 6291460
  133.2 120.2 %all-gather.6.cloned.1.call-start = ((), (), s32[]{:S(2)}) async-start(), calls=%async_computation.10 | async-start | bytes 3145728 | tf_op jit(solution)/shard_map/all_gather | solution.py:139
  134.0 154.0 %all-gather.8.cloned.1.call-start = ((), (), s32[]{:S(2)}) async-start(), calls=%async_computation.11 | async-start | bytes 3145728 | tf_op jit(solution)/shard_map/all_gather | solution.py:140
  134.5 260.7 %all-reduce.24.cloned.1.call-start = ((), (), s32[]{:S(2)}) async-start(), calls=%async_computation.12 | async-start | bytes 4194304 | tf_op jit(solution)/shard_map/psum | solution.py:55
  135.5 89.7 %copy-start.36 = (f32[1,1024]{1,0:T(1,128)}, f32[1,1024]{1,0:T(1,128)S(1)}, u32[]{:S(2)}) copy-start(f32[1,1024]{1,0:T(1,128)S(1)} %get-tuple-element.442) | copy-start | bytes 12292
  222.2 31.2 %copy-start.35 = (f32[1,1024]{1,0:T(1,128)S(1)}, f32[1,1024]{1,0:T(1,128)}, u32[]{:S(2)}) copy-start(f32[1,1024]{1,0:T(1,128)} %get-tuple-element.443) | copy-start | bytes 12292
  222.2 31.2 %copy-start.51 = (f32[1,1024]{1,0:T(1,128)S(1)}, f32[1,1024]{1,0:T(1,128)}, u32[]{:S(2)}) copy-start(f32[1,1024]{1,0:T(1,128)} %get-tuple-element.445) | copy-start | bytes 12292
  253.4 34.5 %copy-start.10 = (bf16[2,512,1024]{2,1,0:T(8,128)(2,1)S(1)}, bf16[2,512,1024]{2,1,0:T(8,128)(2,1)}, u32[]{:S(2)}) copy-start(bf16[2,512,1024]{2,1,0:T(8,128)(2,1)} %param.31) | copy-start | bytes 6291460
  253.4 34.5 %copy-start.50 = (f32[1024]{0:T(1024)S(1)}, f32[1024]{0:T(1024)}, u32[]{:S(2)}) copy-start(f32[1024]{0:T(1024)} %param.26) | copy-start | bytes 12292
  287.9 17.3 %copy-start.53 = (bf16[1024,1024]{1,0:T(8,128)(2,1)S(1)}, bf16[1024,1024]{1,0:T(8,128)(2,1)}, u32[]{:S(2)}) copy-start(bf16[1024,1024]{1,0:T(8,128)(2,1)} %all-gather.6.cloned.1.call-done) | copy-start | bytes 6291460
  308.9 309.7 %reduce-scatter.7.cloned.1.call-start = ((), (), s32[]{:S(2)}) async-start(), calls=%async_computation.14 | async-start | bytes 786432 | tf_op jit(solution)/shard_map/reduce_scatter | solution.py:266
  408.5 210.2 %reduce-scatter.11.cloned.1.call-start = ((), (), s32[]{:S(2)}) async-start(), calls=%async_computation.16 | async-start | bytes 3145728 | tf_op jit(solution)/shard_map/reduce_scatter | solution.py:272
  422.5 12.3 %all-to-all-start.2 = ((bf16[2,512,256]{1,0,2:T(2,128)(2,1)}), bf16[2,512,256]{1,0,2:T(2,128)(2,1)S(1)}, u32[]{:S(2)}, u32[]{:S(2)}) async-start(bf16[2,512,256]{1,0,2:T(2,128)(2,1)} %copy.83), calls=%async_computation.2 | async-start | bytes 1048576 | tf_op jit(solution)/shard_map/all_to_all | solution.py:211
  426.0 192.7 %reduce-scatter.9.cloned.1.call-start = ((), (), s32[]{:S(2)}) async-start(), calls=%async_computation.15 | async-start | bytes 3145728 | tf_op jit(solution)/shard_map/reduce_scatter | solution.py:269
  432.9 197.7 %reduce-scatter.5.cloned.1.call-start = ((), (), s32[]{:S(2)}) async-start(), calls=%async_computation.13 | async-start | bytes 2359296 | tf_op jit(solution)/shard_map/reduce_scatter | solution.py:263
  606.2 182.3 %all-reduce.26.cloned.1.call-start = ((), (), s32[]{:S(2)}) async-start(), calls=%async_computation.17 | async-start | bytes 8388608 | tf_op jit(solution)/shard_map/psum | solution.py:55
  606.3 5.4 copy-start.14
  606.3 5.4 copy-start.54
  614.8 173.7 %copy-start.2 = (bf16[2,512,1024]{2,1,0:T(8,128)(2,1)S(1)}, bf16[2,512,1024]{2,1,0:T(8,128)(2,1)}, u32[]{:S(2)}) copy-start(bf16[2,512,1024]{2,1,0:T(8,128)(2,1)} %param.20) | copy-start | bytes 6291460
  614.8 173.7 %copy-start.32 = (f32[1,4,2,128]{3,1,2,0:T(4,128)S(1)}, f32[1,4,2,128]{3,1,2,0:T(4,128)}, u32[]{:S(2)}) copy-start(f32[1,4,2,128]{3,1,2,0:T(4,128)} %copy-done.31) | copy-start | bytes 12292
  614.9 173.7 %copy-start.34 = (f32[1,1024]{1,0:T(1,128)S(1)}, f32[1,1024]{1,0:T(1,128)}, u32[]{:S(2)}) copy-start(f32[1,1024]{1,0:T(1,128)} %copy-done.33) | copy-start | bytes 12292
  614.9 244.4 %all-reduce.28.cloned.1.call-start = ((), (), s32[]{:S(2)}) async-start(), calls=%async_computation.18 | async-start | bytes 6291456 | tf_op jit(solution)/shard_map/psum | solution.py:277
  617.3 174.4 %copy-start.41 = (f32[1,4,2,128]{3,1,2,0:T(4,128)S(1)}, f32[1,4,2,128]{3,1,2,0:T(4,128)}, u32[]{:S(2)}) copy-start(f32[1,4,2,128]{3,1,2,0:T(4,128)} %copy-done.40) | copy-start | bytes 12292
  617.3 174.4 %copy-start.44 = (f32[1024]{0:T(1024)S(1)}, f32[1024]{0:T(1024)}, u32[]{:S(2)}) copy-start(f32[1024]{0:T(1024)} %get-tuple-element.296) | copy-start | bytes 12292
  617.3 174.4 %copy-start.39 = (f32[1024]{0:T(1024)S(1)}, f32[1024]{0:T(1024)}, u32[]{:S(2)}) copy-start(f32[1024]{0:T(1024)} %copy-done.38) | copy-start | bytes 12292
  788.5 5.9 copy-start.43
  788.5 5.9 copy-start.52
  788.6 32.2 %copy-start.37 = (f32[1,1024]{1,0:T(1,128)S(1)}, f32[1,1024]{1,0:T(1,128)}, u32[]{:S(2)}) copy-start(f32[1,1024]{1,0:T(1,128)} %copy-done.36) | copy-start | bytes 12292
  788.6 32.2 %copy-start.45 = (f32[1,1024]{1,0:T(1,128)S(1)}, f32[1,1024]{1,0:T(1,128)}, u32[]{:S(2)}) copy-start(f32[1,1024]{1,0:T(1,128)} %get-tuple-element.441) | copy-start | bytes 12292
  859.2 7.2 copy-start.27
  (25 other events, 62.0 us)
Sparse Core Ops, SparseCore 0:
  10.1 29.8 all-gather.3
  133.3 86.3 all-reduce.21
  221.2 32.1 all-gather.5
  254.8 33.0 all-gather.7
  309.1 86.1 all-reduce.23
  408.7 13.6 reduce-scatter.6
  424.6 31.8 reduce-scatter.10
  458.8 31.8 reduce-scatter.8
  606.3 24.2 reduce-scatter.4
  633.5 155.0 all-reduce.25
  791.1 68.0 all-reduce.27
where the time goes:
time: 888 us; the launch traced here: 875 us
  waiting for transfers between devices  461 us (52%)
  local copies, waits for them, and re-layouts  130 us (15%)
  matrix products  113 us (13%)
  other arithmetic  71.1 us (8%)
  blocking collectives  60.2 us (7%)
  starting transfers between devices  23.8 us (3%)
  between operations  15.3 us (2%)
    psum x3, waiting for transfers between devices, tp_whole(): return lax.psum(partial_sum.astype(jnp.bfloat16), 'tp').astype(jnp.float32)  316 us
    dynamic_update_slice x4, local copies, waits for them, and re-layouts, shards(): lax.map(backward_group, (grouped[0], grouped[1], grouped[2], grad_grouped...  51.9 us
    psum x1, waiting for transfers between devices, shards(): lax.psum(shard_qkv.astype(jnp.bfloat16), 'ctx').astype(jnp.float32)  31.4 us
    unnamed x122, local copies, waits for them, and re-layouts  28.2 us
    all_gather x1, waiting for transfers between devices, shards(): lax.all_gather(w_up, 'fsdp', axis=0, tiled=True)  28.2 us
    all_gather x1, waiting for transfers between devices, shards(): lax.all_gather(w_down, 'fsdp', axis=1, tiled=True)  27.1 us
    psum x1, blocking collectives, shards(): lax.psum((norm_vectors[0:2], norm_vectors[2:4], norm_vectors[4:6], grad_b...  26.2 us
    all_to_all x1, blocking collectives, shards(): lax.all_to_all(grad_heads, 'ctx', split_axis=2, concat_axis=3, tiled=True)  24.7 us
  transfers between devices with their start and end apart: 14, of which 10 were waited for; matrix products, arithmetic and copies ran while one was open for 24% of the time, Pallas kernels for 0%

commit v1 on v0

--- a/solution.py
+++ b/solution.py
@@ -9,6 +9,11 @@
 ROT = 20
 QBLK = 512
 EPSILON = 1e-06
+
+
+def wall_step_on(work_x, axis_name):
+    w1 = jnp.sum(jax.lax.all_gather(work_x, axis_name), axis=0)
+    return w1
 
 
 def layer_norm(values, gain_vec, shift_vec):
@@ -52,7 +57,7 @@
 
 
 def tp_whole(partial_sum):
-    return lax.psum(partial_sum.astype(jnp.bfloat16), "tp").astype(jnp.float32)
+    return wall_step_on(partial_sum.astype(jnp.bfloat16), "tp").astype(jnp.float32)
 
 
 def attend_group(operands):

time: 888 us -> 1250 us (1.41)
  waiting for transfers between devices: 461 us -> 801 us
  other arithmetic: 71.1 us -> 105 us
    all_gather x0 -> x4, waiting for transfers between devices: none -> 565 us  [wall_step_on(): w1 = jnp.sum(jax.lax.all_gather(work_x, axis_name), axis=0)]
    psum x3 -> x0, waiting for transfers between devices: 316 us -> none  [tp_whole(): return lax.psum(partial_sum.astype(jnp.bfloat16), 'tp').astype(jnp.float32)]
    reduce_scatter x1, waiting for transfers between devices: 0.02 us -> 34.2 us  [shards(): lax.psum_scatter(grad_up.astype(jnp.bfloat16), 'fsdp', scatter_dimension=...]
    reduce_sum x1 -> x4, other arithmetic: 2.12 us -> 30.1 us  [wall_step_on(): w1 = jnp.sum(jax.lax.all_gather(work_x, axis_name), axis=0)]
    reduce_scatter x1, waiting for transfers between devices: 0.02 us -> 17.5 us  [shards(): lax.psum_scatter(grad_proj.astype(jnp.bfloat16), 'fsdp', scatter_dimensio...]
    reduce_scatter x1, waiting for transfers between devices: 11.9 us -> 28.8 us  [shards(): lax.psum_scatter(grad_qkv.astype(jnp.bfloat16), 'fsdp', scatter_dimension...]
    reduce_scatter x1, waiting for transfers between devices: 0.02 us -> 13.9 us  [shards(): lax.psum_scatter(grad_down.astype(jnp.bfloat16), 'fsdp', scatter_dimensio...]
    psum x1, waiting for transfers between devices: 31.4 us -> 44.8 us  [shards(): lax.psum(shard_qkv.astype(jnp.bfloat16), 'ctx').astype(jnp.float32)]
  transfers between devices with their start and end apart: 14 -> 15, of which waited for: 10 -> 14; matrix products, arithmetic and copies ran while one was open for 24% -> 6% of each run, Pallas kernels for 0% -> 0%
where the time goes in v1:
time: 1250 us; the launch traced here: 1230 us
  waiting for transfers between devices  801 us (64%)
  local copies, waits for them, and re-layouts  128 us (10%)
  matrix products  113 us (9%)
  other arithmetic  105 us (8%)
  blocking collectives  58.8 us (5%)
  between operations  15.4 us (1%)
    all_gather x4, waiting for transfers between devices, wall_step_on(): w1 = jnp.sum(jax.lax.all_gather(work_x, axis_name), axis=0)  565 us
    dynamic_update_slice x4, local copies, waits for them, and re-layouts, shards(): lax.map(backward_group, (grouped[0], grouped[1], grouped[2], grad_grouped...  51.9 us
    psum x1, waiting for transfers between devices, shards(): lax.psum(shard_qkv.astype(jnp.bfloat16), 'ctx').astype(jnp.float32)  44.8 us
    reduce_scatter x1, waiting for transfers between devices, shards(): lax.psum_scatter(grad_up.astype(jnp.bfloat16), 'fsdp', scatter_dimension=...  34.2 us
    reduce_sum x4, other arithmetic, wall_step_on(): w1 = jnp.sum(jax.lax.all_gather(work_x, axis_name), axis=0)  30.1 us
    reduce_scatter x1, waiting for transfers between devices, shards(): lax.psum_scatter(grad_qkv.astype(jnp.bfloat16), 'fsdp', scatter_dimension...  28.8 us
    unnamed x132, local copies, waits for them, and re-layouts  28.1 us
    all_gather x1, waiting for transfers between devices, shards(): lax.all_gather(w_down, 'fsdp', axis=1, tiled=True)  28 us
  transfers between devices with their start and end apart: 15, of which 14 were waited for; matrix products, arithmetic and copies ran while one was open for 6% of the time, Pallas kernels for 0%

profile of v1, /device:TPU:0, one launch (start us, length us, event | category | flops | bytes accessed | tf_op | source)
XLA Modules:
  0.0 1234.4 jit_solution(3005982965014301354)
XLA Ops:
  17.3 22.8 %all-gather.12.cloned.1.call-done = bf16[3,1024,256]{1,2,0:T(8,128)(2,1)} async-done(((bf16[3,512,256]{1,2,0:T(8,128)(2,1)}), bf16[3,1024,256]{1,2,0:T(8,128)(2,1)}) %all-gather.12.cloned.1.call-update) | async-done | bytes 1572880 | tf_op jit(solution)/shard_map/all_gather | solution.py:142
  40.1 3.9 add_bitcast_fusion
  54.5 4.0 all-to-all-start
  58.6 20.0 %all-to-all-done = bf16[3,2,512,256]{2,1,0,3:T(2,128)(2,1)S(1)} async-done(((bf16[3,2,512,256]{2,1,0,3:T(2,128)(2,1)}), bf16[3,2,512,256]{2,1,0,3:T(2,128)(2,1)S(1)}, u32[]{:S(2)}, u32[]{:S(2)}) %all-to-all-start) | async-done | bytes 1572896 | tf_op jit(solution)/shard_map/all_to_all | solution.py:166
  83.3 27.2 %while.54 = (s32[]{:T(128)}, bf16[2,4,512,64]{2,3,1,0:T(8,128)(2,1)}, f32[2,4,512]{2,1,0:T(4,128)S(1)}, bf16[2,2048,64]{2,1,0:T(8,128)(2,1)S(1)}, bf16[2,2048,64...) while((s32[]{:T(128)}, ...), condition=%wide.region_7.8_spmd, body=%wide.region_2.7_spmd.sunk | while | flops 277904896 | bytes 20156772 | solution.py:173
  84.6 11.4 while.57
  98.2 11.4 while.57
  114.6 3.5 all-to-all-start.1
  118.2 9.3 all_gather.41
  133.5 148.6 %all-gather.18.cloned.1.call-done = bf16[4096,1024]{1,0:T(8,128)(2,1)} async-done(((bf16[1024,1024]{1,0:T(8,128)(2,1)}), bf16[4096,1024]{1,0:T(8,128)(2,1)}) %all-gather.18.cloned.1.call-update) | async-done | bytes 8388624 | tf_op jit(solution)/shard_map/all_gather | solution.py:15
  282.0 7.6 reduce_sum.221
  297.8 17.1 %all-gather.14.cloned.1.call-done = bf16[1024,1024]{1,0:T(8,128)(2,1)} async-done(((bf16[512,1024]{1,0:T(8,128)(2,1)}), bf16[1024,1024]{1,0:T(8,128)(2,1)}) %all-gather.14.cloned.1.call-update) | async-done | bytes 2097168 | tf_op jit(solution)/shard_map/all_gather | solution.py:144
  314.9 6.5 fusion.85
  321.4 28.0 %all-gather.16.cloned.1.call-done = bf16[1024,1024]{1,0:T(8,128)(2,1)} async-done(((bf16[1024,512]{1,0:T(8,128)(2,1)}), bf16[1024,1024]{1,0:T(8,128)(2,1)}) %all-gather.16.cloned.1.call-update) | async-done | bytes 2097168 | tf_op jit(solution)/shard_map/all_gather | solution.py:145
  349.4 15.7 %convert_reduce_fusion.2 = (f32[1024]{0:T(1024)}, bf16[1024,1024]{1,0:T(8,128)(2,1)}, f32[1024,1024]{1,0:T(8,128)S(1)}) fusion(f32[1024,1024]{1,0:T(8,128)} %fusion.85, f32[1024]{0:T(1024)S(1)} %copy-done.56, bf16[1024,1024]{1,0:T(8,128)(2,1)} %bitcast.298, bf16[1024,1024]{1,0:T(8,128)(2,1)} %all-gather.16.cloned.1.call-done), kind=kOutput, calls=%fused_computation.85 | convolution fusion | flops 2226125824 | bytes 14688256 | tf_op jit(solution)/shard_map/dot_general | solution.py:54
  367.6 3.7 convolution_convert_fusion.3
  371.6 5.9 convolution_convert_fusion.2
  377.6 143.6 %all-gather.20.cloned.1.call-done = bf16[4096,1024]{1,0:T(8,128)(2,1)} async-done(((bf16[1024,1024]{1,0:T(8,128)(2,1)}), bf16[4096,1024]{1,0:T(8,128)(2,1)}) %all-gather.20.cloned.1.call-update) | async-done | bytes 8388624 | tf_op jit(solution)/shard_map/all_gather | solution.py:15
  521.1 7.5 reduce_sum.227
  528.6 142.3 %all-gather.22.cloned.1.call-done = bf16[4096,1024]{1,0:T(8,128)(2,1)} async-done(((bf16[1024,1024]{1,0:T(8,128)(2,1)}), bf16[4096,1024]{1,0:T(8,128)(2,1)}) %all-gather.22.cloned.1.call-update) | async-done | bytes 8388624 | tf_op jit(solution)/shard_map/all_gather | solution.py:15
  671.0 7.5 reduce_sum.228
  678.4 5.5 multiply_reduce_fusion.2
  690.9 5.0 convert_reduce_fusion.4
  701.8 8.3 all-to-all-done.2
  711.5 103.5 %while.56 = (s32[]{:T(128)}, bf16[2,2048,64]{2,0,1:T(2,128)(2,1)}, bf16[2,2048,64]{1,2,0:T(8,128)(2,1)}, bf16[2,2048,64]{1,2,0:T(8,128)(2,1)}, bf16[2,2048,64]{2...) while((s32[]{:T(128)}, bf16[2,2048,64]{2,0,1:T(2,128)(2,1)}, ...), condition=%wide.region_19.20_spmd, body=%wide.region_15.19_spmd.sunk | while | flops 680164864 | bytes 41838996 | solution.py:222
  715.8 20.0 %while.58 = (s32[]{:T(128)}, f32[2048,64]{0,1:T(8,128)S(1)}, f32[2048,64]{0,1:T(8,128)S(1)}, f32[4,512,64]{1,2,0:T(8,128)}, bf16[4,512,64]{2,1,0:T(8,128)(2,1)S(...) while((s32[]{:T(128)}, f32[2048,64]{0,1:T(8,128)S(1)}, ...), condition=%wide.region_18.18_spmd.clone, body=%wide.region_16.17_spmd.clone.sunk | while | flops 680164864 | bytes 35530900 | solution.py:116
  737.2 25.1 %dynamic_update_slice.47 = bf16[2,2048,64]{2,0,1:T(2,128)(2,1)} dynamic-update-slice(bf16[2,2048,64]{2,0,1:T(2,128)(2,1)} %get-tuple-element.803, f32[1,2048,64]{2,0,1:T(1,128)S(1)} %bitcast.284, s32[]{:T(128)S(6)} %copy.191, s32[]{:T(128)} %constant.78.clone.1..sunk.2, s32[]{:T(128)} %constant.78.clone.1..sunk.2) | dynamic-update-slice | bytes 1048580 | tf_op jit(solution)/shard_map/while/body/jit(dynamic_update_index_in_dim)/dynamic_update_slice | solution.py:222
  767.6 20.0 %while.58 = (s32[]{:T(128)}, f32[2048,64]{0,1:T(8,128)S(1)}, f32[2048,64]{0,1:T(8,128)S(1)}, f32[4,512,64]{1,2,0:T(8,128)}, bf16[4,512,64]{2,1,0:T(8,128)(2,1)S(...) while((s32[]{:T(128)}, f32[2048,64]{0,1:T(8,128)S(1)}, ...), condition=%wide.region_18.18_spmd.clone, body=%wide.region_16.17_spmd.clone.sunk | while | flops 680164864 | bytes 35530900 | solution.py:116
  789.0 25.1 %dynamic_update_slice.47 = bf16[2,2048,64]{2,0,1:T(2,128)(2,1)} dynamic-update-slice(bf16[2,2048,64]{2,0,1:T(2,128)(2,1)} %get-tuple-element.803, f32[1,2048,64]{2,0,1:T(1,128)S(1)} %bitcast.284, s32[]{:T(128)S(6)} %copy.191, s32[]{:T(128)} %constant.78.clone.1..sunk.2, s32[]{:T(128)} %constant.78.clone.1..sunk.2) | dynamic-update-slice | bytes 1048580 | tf_op jit(solution)/shard_map/while/body/jit(dynamic_update_index_in_dim)/dynamic_update_slice | solution.py:222
  814.9 3.6 copy.146
  818.5 3.6 copy.145
  822.1 7.2 fusion.84
  832.6 24.6 %all_to_all.57 = bf16[4,2,98304]{2,1,0:T(2,128)(2,1)} all-to-all(bf16[4,2,98304]{2,1,0:T(2,128)(2,1)} %reshape.506), channel_id=1, replica_groups=mesh['fsdp'=2,'ctx'=4,'tp'=4] {'ctx'}, dimensions={0} | all-to-all | bytes 3145728 | tf_op jit(solution)/shard_map/all_to_all | solution.py:232
  857.2 3.8 reshape.507
  861.0 6.4 copy.92
  882.3 4.8 bitcast_convert_fusion
  887.2 5.3 convolution_convert_fusion
  892.8 6.6 convolution_convert_fusion.1
  899.4 4.6 fusion.63
  904.1 130.1 %all-gather.24.cloned.1.call-done = bf16[4096,1024]{1,0:T(8,128)(2,1)} async-done(((bf16[1024,1024]{1,0:T(8,128)(2,1)}), bf16[4096,1024]{1,0:T(8,128)(2,1)}) %all-gather.24.cloned.1.call-update) | async-done | bytes 8388624 | tf_op jit(solution)/shard_map/all_gather | solution.py:15
  1034.2 7.6 reduce_sum.235
  1047.4 3.6 fusion.66
  1052.6 13.9 %reduce-scatter.11.cloned.1.call-done = bf16[1024,512]{1,0:T(8,128)(2,1)} async-done(((bf16[1024,1024]{1,0:T(8,128)(2,1)}), bf16[1024,512]{1,0:T(8,128)(2,1)}) %reduce-scatter.11.cloned.1.call-update) | async-done | bytes 1048592 | tf_op jit(solution)/shard_map/reduce_scatter | solution.py:277
  1066.5 34.2 %reduce-scatter.9.cloned.1.call-done = bf16[512,1024]{1,0:T(8,128)(2,1)} async-done(((bf16[1024,1024]{1,0:T(8,128)(2,1)}), bf16[512,1024]{1,0:T(8,128)(2,1)}) %reduce-scatter.9.cloned.1.call-update) | async-done | bytes 1048592 | tf_op jit(solution)/shard_map/reduce_scatter | solution.py:274
  1100.7 28.8 %reduce-scatter.5.cloned.1.call-done = bf16[3,512,256]{1,2,0:T(8,128)(2,1)} async-done(((bf16[3,1024,256]{1,2,0:T(8,128)(2,1)}), bf16[3,512,256]{1,2,0:T(8,128)(2,1)}) %reduce-scatter.5.cloned.1.call-update) | async-done | bytes 786448 | tf_op jit(solution)/shard_map/reduce_scatter | solution.py:268
  1129.6 17.5 %reduce-scatter.7.cloned.1.call-done = bf16[256,512]{1,0:T(8,128)(2,1)} async-done(((bf16[256,1024]{1,0:T(8,128)(2,1)}), bf16[256,512]{1,0:T(8,128)(2,1)}) %reduce-scatter.7.cloned.1.call-update) | async-done | bytes 262160 | tf_op jit(solution)/shard_map/reduce_scatter | solution.py:271
  1148.8 24.9 %all-reduce.14 = (f32[3,256]{1,0:T(4,128)}, f32[1024]{0:T(1024)}, f32[2,1024]{1,0:T(2,128)}, f32[2,1024]{1,0:T(2,128)}, f32[2,1024]{1,0:T(2,128)}) all-reduce(f32[3,256]{1,0:T(4,128)S(1)} %convert_reduce_fusion.3, f32[1024]{0:T(1024)S(1)} %copy-done.57, ...), channel_id=1, replica_groups=mesh['fsdp'=2,'ctx'=4,'tp'=4] {'fsdp','ctx'}, use_global_device_ids=true, to_apply=%region_26.27 | all-reduce | flops 7936 | bytes 63488 | tf_op jit(solution)/shard_map/psum | solution.py:287
  1173.7 44.8 %all-reduce.18.cloned.1.call-done = (bf16[3,512,256]{1,2,0:T(8,128)(2,1)}, bf16[256,512]{1,0:T(8,128)(2,1)}, bf16[512,1024]{1,0:T(8,128)(2,1)}, bf16[1024,512]{1,0:T(8,128)(2,1)}) async-done(((bf16[3,512,256]{1,2,0:T(8,128)(2,1)}, bf16[256,512]{1,0:T(8,128)(2,1)}, bf16[512,1024]{1,0:T(8,128)(2,1)}, bf16[1024,512]{1,0:T(8,128)(2,1)}), (bf16[3,512,256]{1,2,0:T(8,128)(2,1)}, bf16[256,512]{1,0:T(8,128)(2,1)}, ...) | async-done | bytes 3145744 | tf_op jit(solution)/shard_map/psum | solution.py:282
  (371 shorter events, 176.2 us)
Async XLA Ops:
  7.2 4.5 copy-start
  7.2 5.8 copy-start.52
  7.2 5.8 copy-start.53
  7.2 6.4 copy-start.54
  7.2 32.9 %all-gather.12.cloned.1.call-start = ((), (), s32[]{:S(2)}) async-start(), calls=%async_computation.8 | async-start | bytes 2359296 | tf_op jit(solution)/shard_map/all_gather | solution.py:142
  11.7 28.4 %copy-start.59 = (f32[3,256]{1,0:T(4,128)S(1)}, f32[3,256]{1,0:T(4,128)}, u32[]{:S(2)}) copy-start(f32[3,256]{1,0:T(4,128)} %param.23) | copy-start | bytes 9220
  15.1 30.8 %copy-start.19 = (f32[1024,10]{0,1:T(8,128)}, f32[1024,10]{0,1:T(8,128)S(1)}, u32[]{:S(2)}) copy-start(f32[1024,10]{0,1:T(8,128)S(1)} %get-tuple-element.436) | copy-start | bytes 122884
  15.1 30.8 %copy-start.21 = (f32[1024,10]{0,1:T(8,128)}, f32[1024,10]{0,1:T(8,128)S(1)}, u32[]{:S(2)}) copy-start(f32[1024,10]{0,1:T(8,128)S(1)} %get-tuple-element.437) | copy-start | bytes 122884
  15.1 30.8 %copy-start.23 = (f32[1024,10]{0,1:T(8,128)}, f32[1024,10]{0,1:T(8,128)S(1)}, u32[]{:S(2)}) copy-start(f32[1024,10]{0,1:T(8,128)S(1)} %get-tuple-element.438) | copy-start | bytes 122884
  15.1 30.8 %copy-start.25 = (f32[1024,10]{0,1:T(8,128)}, f32[1024,10]{0,1:T(8,128)S(1)}, u32[]{:S(2)}) copy-start(f32[1024,10]{0,1:T(8,128)S(1)} %get-tuple-element.457) | copy-start | bytes 122884
  15.1 30.8 %copy-start.27 = (f32[1024,10]{0,1:T(8,128)}, f32[1024,10]{0,1:T(8,128)S(1)}, u32[]{:S(2)}) copy-start(f32[1024,10]{0,1:T(8,128)S(1)} %get-tuple-element.458) | copy-start | bytes 122884
  15.1 30.8 %copy-start.29 = (f32[1024,10]{0,1:T(8,128)}, f32[1024,10]{0,1:T(8,128)S(1)}, u32[]{:S(2)}) copy-start(f32[1024,10]{0,1:T(8,128)S(1)} %get-tuple-element.459) | copy-start | bytes 122884
  54.5 24.0 %all-to-all-start = ((bf16[3,2,512,256]{2,1,0,3:T(2,128)(2,1)}), bf16[3,2,512,256]{2,1,0,3:T(2,128)(2,1)S(1)}, u32[]{:S(2)}, u32[]{:S(2)}) async-start(bf16[3,2,512,256]{2,1,0,3:T(2,128)(2,1)} %pad_maximum_fusion.1), calls=%async_computation | async-start | bytes 3145728 | tf_op jit(solution)/shard_map/all_to_all | solution.py:166
  84.6 11.4 copy-start.37
  98.2 11.4 copy-start.37
  110.5 18.6 %copy-start.9 = (bf16[2,2048,64]{2,1,0:T(8,128)(2,1)}, bf16[2,2048,64]{2,1,0:T(8,128)(2,1)S(1)}, u32[]{:S(2)}) copy-start(bf16[2,2048,64]{2,1,0:T(8,128)(2,1)S(1)} %get-tuple-element.847) | copy-start | bytes 1572868
  110.5 7.7 copy-start.39
  114.6 12.8 %all-to-all-start.1 = ((bf16[4,2,32768]{2,1,0:T(2,128)(2,1)}), bf16[4,2,32768]{2,1,0:T(2,128)(2,1)S(1)}, u32[]{:S(2)}, u32[]{:S(2)}) async-start(bf16[4,2,32768]{2,1,0:T(2,128)(2,1)} %reshape.504), calls=%async_computation.1 | async-start | bytes 1048576 | tf_op jit(solution)/shard_map/all_to_all | solution.py:179
  118.1 163.9 %all-gather.18.cloned.1.call-start = ((), (), s32[]{:S(2)}) async-start(), calls=%async_computation.15 | async-start | bytes 10485760 | tf_op jit(solution)/shard_map/all_gather | solution.py:15
  129.0 4.4 copy-start.55
  132.1 182.8 %all-gather.14.cloned.1.call-start = ((), (), s32[]{:S(2)}) async-start(), calls=%async_computation.9 | async-start | bytes 3145728 | tf_op jit(solution)/shard_map/all_gather | solution.py:144
  132.8 216.6 %all-gather.16.cloned.1.call-start = ((), (), s32[]{:S(2)}) async-start(), calls=%async_computation.10 | async-start | bytes 3145728 | tf_op jit(solution)/shard_map/all_gather | solution.py:145
  133.4 387.7 %all-gather.20.cloned.1.call-start = ((), (), s32[]{:S(2)}) async-start(), calls=%async_computation.16 | async-start | bytes 10485760 | tf_op jit(solution)/shard_map/all_gather | solution.py:15
  282.0 7.6 copy-start.1
  297.8 51.6 %copy-start.56 = (f32[1024]{0:T(1024)S(1)}, f32[1024]{0:T(1024)}, u32[]{:S(2)}) copy-start(f32[1024]{0:T(1024)} %param.26) | copy-start | bytes 12292
  349.4 15.7 %copy-start.14 = (f32[1024,1024]{1,0:T(8,128)S(1)}, f32[1024,1024]{1,0:T(8,128)}, u32[]{:S(2)}) copy-start(f32[1024,1024]{1,0:T(8,128)} %fusion.85) | copy-start | bytes 12582916
  371.4 299.6 %all-gather.22.cloned.1.call-start = ((), (), s32[]{:S(2)}) async-start(), calls=%async_computation.17 | async-start | bytes 10485760 | tf_op jit(solution)/shard_map/all_gather | solution.py:15
  678.4 5.5 copy-start.4
  678.4 5.5 copy-start.7
  678.4 5.9 copy-start.11
  697.8 12.3 all-to-all-start.2
  701.3 332.9 %all-gather.24.cloned.1.call-start = ((), (), s32[]{:S(2)}) async-start(), calls=%async_computation.18 | async-start | bytes 10485760 | tf_op jit(solution)/shard_map/all_gather | solution.py:15
  874.5 4.0 copy-start.32
  882.3 4.9 copy-start.12
  887.1 179.4 %reduce-scatter.11.cloned.1.call-start = ((), (), s32[]{:S(2)}) async-start(), calls=%async_computation.14 | async-start | bytes 3145728 | tf_op jit(solution)/shard_map/reduce_scatter | solution.py:277
  892.5 6.9 copy-start.16
  892.5 208.2 %reduce-scatter.9.cloned.1.call-start = ((), (), s32[]{:S(2)}) async-start(), calls=%async_computation.13 | async-start | bytes 3145728 | tf_op jit(solution)/shard_map/reduce_scatter | solution.py:274
  899.3 230.2 %reduce-scatter.5.cloned.1.call-start = ((), (), s32[]{:S(2)}) async-start(), calls=%async_computation.11 | async-start | bytes 2359296 | tf_op jit(solution)/shard_map/reduce_scatter | solution.py:268
  904.0 243.0 %reduce-scatter.7.cloned.1.call-start = ((), (), s32[]{:S(2)}) async-start(), calls=%async_computation.12 | async-start | bytes 786432 | tf_op jit(solution)/shard_map/reduce_scatter | solution.py:271
  1034.2 7.6 copy-start.2
  1034.2 7.6 copy-start.43
  1034.2 7.6 copy-start.45
  1051.1 97.3 %copy-start.6 = (bf16[1024,1024]{1,0:T(8,128)(2,1)S(1)}, bf16[1024,1024]{1,0:T(8,128)(2,1)}, u32[]{:S(2)}) copy-start(bf16[1024,1024]{1,0:T(8,128)(2,1)} %reduce_sum.235) | copy-start | bytes 6291460
  1052.6 96.2 %copy-start.49 = (f32[1024]{0:T(1024)S(1)}, f32[1024]{0:T(1024)}, u32[]{:S(2)}) copy-start(f32[1024]{0:T(1024)} %get-tuple-element.388) | copy-start | bytes 12292
  1052.6 96.2 %copy-start.48 = (f32[1024]{0:T(1024)S(1)}, f32[1024]{0:T(1024)}, u32[]{:S(2)}) copy-start(f32[1024]{0:T(1024)} %get-tuple-element.290) | copy-start | bytes 12292
  1052.6 96.2 %copy-start.57 = (f32[1024]{0:T(1024)S(1)}, f32[1024]{0:T(1024)}, u32[]{:S(2)}) copy-start(f32[1024]{0:T(1024)} %get-tuple-element.365) | copy-start | bytes 12292
  1052.6 165.9 %all-reduce.18.cloned.1.call-start = ((), (), s32[]{:S(2)}) async-start(), calls=%async_computation.19 | async-start | bytes 6291456 | tf_op jit(solution)/shard_map/psum | solution.py:282
  1218.5 7.2 copy-start.31
  (29 other events, 72.8 us)
Sparse Core Ops, SparseCore 0:
  10.1 29.8 all-gather.11
  132.2 149.7 all-gather.17
  283.6 31.2 all-gather.13
  316.3 33.0 all-gather.15
  371.5 149.5 all-gather.19
  523.1 147.7 all-gather.21
  887.2 146.8 all-gather.23
  1036.4 30.0 reduce-scatter.10
  1068.8 31.8 reduce-scatter.8
  1103.4 26.1 reduce-scatter.4
  1132.4 14.6 reduce-scatter.6
  1149.5 68.9 all-reduce.17
